TPU v7x, 32 devices: a whole 2x2x4 slice. The times are simulated.
32 devices in a mesh: dp: 4 (over x, core), section: 2 (over y), mp: 4 (over z).
Axes of the slice: x: 2, y: 2, z: 4, core: 2. Of those that a mesh axis runs over, the one named last changes fastest.
Arguments:
- micro_inputs: bfloat16 [8, 64, 4096], P(('dp', 'section'), None, 'mp'), parts along dimension 0, may hold values from -6 to 6
- qkv_weight: bfloat16 [2, 4096, 3, 2048], P('section', None, None, 'mp'), may hold values from -0.09375 to 0.09375
- out_weight: bfloat16 [2, 2048, 4096], P('section', None, 'mp'), may hold values from -0.125 to 0.125
- norm_gain: bfloat16 [2, 4096], P('section'), may hold values from 0.099609375 to 1.8984375
- position_bias: float32 [32, 32], P('mp'), may hold values from -3 to 280
Outputs:
- encoded: bfloat16 [8, 64, 4096], P(('dp', 'section'), None, 'mp'), parts along dimension 0
There are 4 independent parts, one for each index of `dp`. A program takes and returns all parts, laid end to end along the dimension named above; an argument that names none is the same for every part. Nothing has to cross between parts.
All inputs are finite; a program needn't handle non-finite values.
Results may differ from a plain program's by a relative error of at most 0.025.
Values may be sent and summed in bfloat16 or wider, within the bound.
A program may use at most 128 MiB of HBM per device.

v0:
```python
import math

import jax
import jax.numpy as jnp
import numpy as np
from jax import lax
from jax.sharding import PartitionSpec as P

REACH = 128


NORM_EPSILON = 0.1


def shifted(x, axis, by):
    peers = lax.axis_size(axis)
    pairs = [(i, i + by) for i in range(peers) if 0 <= i + by < peers]
    return lax.ppermute(x, axis, pairs)


def bucket_table(length, bucket_count, reach_limit):
    offset = np.arange(length)[None, :] - np.arange(length)[:, None]
    half_count = bucket_count // 2
    upper_side = (offset > 0).astype(np.int32) * half_count
    distance = np.abs(offset)
    exact_count = half_count // 2
    scaled = (
        np.log(np.maximum(distance, 1) / exact_count)
        / np.log(reach_limit / exact_count)
        * (half_count - exact_count)
    )
    far_bucket = np.minimum(exact_count + scaled.astype(np.int32), half_count - 1)
    return (upper_side + np.where(distance < exact_count, distance, far_bucket)).astype(np.int32)


def shards(micro_inputs, qkv_weight, out_weight, norm_gain, position_bias):
    sections = lax.axis_size("section")
    section_index = lax.axis_index("section")
    length = micro_inputs.shape[1]
    local_width = micro_inputs.shape[2]
    model_width = qkv_weight.shape[1]
    local_heads = position_bias.shape[0]
    head_size = qkv_weight.shape[3] // local_heads
    weights_qkv = qkv_weight[0].reshape(model_width, 3 * qkv_weight.shape[3])
    weights_out = out_weight[0]
    gain_row = norm_gain[0]
    bucket_count = position_bias.shape[1]
    bucket_grid = jnp.asarray(bucket_table(length, bucket_count, REACH))
    onehot = (
        bucket_grid[:, :, None] == jnp.arange(bucket_count, dtype=jnp.int32)[None, None, :]
    ).astype(jnp.float32)
    score_bias = jnp.einsum("hb,ijb->hij", position_bias, onehot, precision=lax.Precision.HIGHEST)
    score_scale = 1.0 / math.sqrt(head_size)

    def attend(section_in):
        stream = section_in.astype(jnp.float32)
        portion_rows = lax.all_gather(section_in, "mp", axis=1, tiled=True).astype(jnp.float32)
        gain_piece = gain_row.astype(jnp.float32)
        gained_piece = (portion_rows * gain_piece).astype(jnp.bfloat16)
        weight_block = weights_qkv
        running = jnp.dot(gained_piece, weight_block, preferred_element_type=jnp.float32)
        project = running
        squares = jnp.sum(portion_rows * portion_rows, axis=1)
        row_scale = lax.rsqrt(squares / model_width + NORM_EPSILON)[:, None]
        project = (
            (project * row_scale).astype(jnp.bfloat16).reshape(length, 3, local_heads, head_size)
        )
        queries = project[:, 0]
        key_heads = project[:, 1]
        values = project[:, 2]
        scores = (
            jnp.einsum("ihd,jhd->hij", queries, key_heads, preferred_element_type=jnp.float32)
            * score_scale
            + score_bias
        )
        row_max = jnp.max(scores, axis=2, keepdims=True)
        weights = jnp.exp(scores - row_max)
        attn_probs = (weights / jnp.sum(weights, axis=2, keepdims=True)).astype(jnp.bfloat16)
        head_mix = jnp.einsum(
            "hij,jhd->ihd", attn_probs, values, preferred_element_type=jnp.float32
        )
        head_mix = head_mix.astype(jnp.bfloat16).reshape(length, local_heads * head_size)
        weight_block = weights_out
        update = jnp.dot(
            lax.all_gather(head_mix, "mp", axis=1, tiled=True),
            weight_block,
            preferred_element_type=jnp.float32,
        )
        return (stream + update).astype(jnp.bfloat16)

    def forward_step(section_in):
        section_out = attend(section_in)
        return (section_out, shifted(section_out, "section", 1))

    ticks = 2 * sections - 1
    first_section = section_index == 0
    last_section = section_index == sections - 1
    blank = jnp.zeros((length, local_width), jnp.bfloat16)

    def conveyor_tick(tick_index, state_pair):
        belt, received = state_pair
        section_out, received = forward_step(jnp.where(first_section, belt[0], received))
        belt = shifted(belt, "section", -1)
        belt = belt.at[1].set(jnp.where(last_section, section_out, belt[1]))
        return (belt, received)

    belt_start = jnp.stack([micro_inputs[0], blank])
    final_pair = lax.fori_loop(0, ticks, conveyor_tick, (belt_start, blank))
    return final_pair[0][1][None]


def solution(mesh):
    in_specs = (
        P(("dp", "section"), None, "mp"),
        P("section", None, None, "mp"),
        P("section", None, "mp"),
        P("section", None),
        P("mp", None),
    )
    out_specs = P(("dp", "section"), None, "mp")
    return jax.shard_map(shards, mesh=mesh, in_specs=in_specs, out_specs=out_specs, check_vma=False)
```

profile of v0, /device:TPU:0, one launch (start us, length us, event | category | flops | bytes accessed | tf_op | source)
XLA Modules:
  0.0 187.1 jit_solution(15900364324202981719)
XLA Ops:
  0.0 17.0 %copy.17 = bf16[1,4096,3,512]{1,3,2,0:T(8,128)(2,1)} copy(bf16[1,4096,3,512]{3,1,2,0:T(8,128)(2,1)} %param.11) | data formatting | bytes 25165824 | tf_op args[1]
  17.0 16.6 %copy.18 = bf16[4096,1536]{1,0:T(8,128)(2,1)} copy(bf16[4096,1536]{0,1:T(8,128)(2,1)} %bitcast.63) | data formatting | bytes 25165824 | tf_op jit(solution)/shard_map/while | solution.py:108
  34.3 152.1 %while.15 = (s32[]{:T(128)}, bf16[2,64,1024]{2,1,0:T(8,128)(2,1)S(1)}, bf16[64,1024]{1,0:T(8,128)(2,1)S(1)}, pred[]{:T(512)}, pred[]{:T(512)}, /*index=5*/bf16[4...) while((s32[]{:T(128)}, ...), condition=%wide.region_4.0_spmd, body=%wide.region_0.4_spmd.sunk | while | flops 1084494592 | bytes 24294580 | solution.py:108
  34.4 1.3 collective-permute-start
  35.7 17.4 %all_gather.14 = bf16[64,4096]{1,0:T(8,128)(2,1)S(1)} all-gather(bf16[64,1024]{1,0:T(8,128)(2,1)S(1)} %bitcast_select_fusion.2), channel_id=1, replica_groups=mesh['dp'=4,'section'=2,'mp'=4] {'mp'}, dimensions={1}, use_global_device_ids=true | all-gather | bytes 655360 | tf_op jit(solution)/shard_map/while/body/eval_jaxpr/all_gather | solution.py:57
  53.3 6.8 %fusion.46 = bf16[64,1536]{1,0:T(8,128)(2,1)S(1)} fusion(bf16[4096,1536]{1,0:T(8,128)(2,1)} %get-tuple-element.264, bf16[64,4096]{1,0:T(8,128)(2,1)S(1)} %all_gather.14, f32[4096]{0:T(1024)S(1)} %convert_element_type.84, f32[64]{0:T(128)S(1)} %add_rsqrt_fusion.2), kind=kOutput, calls=%fused_computation.2.clone.1 | convolution fusion | flops 806289408 | bytes 13320448 | tf_op jit(solution)/shard_map/while/body/eval_jaxpr/dot_general | solution.py:61
  61.1 16.2 %all_gather.15 = bf16[64,2048]{0,1:T(8,128)(2,1)S(1)} all-gather(bf16[64,512]{0,1:T(8,128)(2,1)S(1)} %bitcast.64), channel_id=1, replica_groups=mesh['dp'=4,'section'=2,'mp'=4] {'mp'}, dimensions={1}, use_global_device_ids=true | all-gather | bytes 327680 | tf_op jit(solution)/shard_map/while/body/eval_jaxpr/all_gather | solution.py:85
  77.4 3.1 %fusion.50 = (bf16[2,64,1024]{2,1,0:T(8,128)(2,1)S(1)}, bf16[64,1024]{1,0:T(8,128)(2,1)S(1)}) fusion(bf16[2,64,1024]{2,1,0:T(8,128)(2,1)S(1)} %collective-permute-done, pred[]{:T(512)} %get-tuple-element.261, bf16[64,2048]{0,1:T(8,128)(2,1)S(1)} %all_gather.15, bf16[2048,1024]{1,0:T(8,128)(2,1)} %get-tuple-element.266, ...), kind=kOutput, calls=%fused_computation.19.clone.1 | convolution fusion | flops 268697600 | bytes 5242881 | tf_op jit(solution)/shard_map/while/body/eval_jaxpr/dot_general | solution.py:84
  80.4 4.3 %collective-permute-start.1 = (bf16[64,1024]{1,0:T(8,128)(2,1)S(1)}, bf16[64,1024]{1,0:T(8,128)(2,1)S(1)}, u32[]{:S(2)}, u32[]{:S(2)}) collective-permute-start(bf16[64,1024]{1,0:T(8,128)(2,1)S(1)} %get-tuple-element.237), channel_id=1, source_target_pairs={{0,4},{1,5},{2,6},{3,7},{8,12},{9,13},{10,14},{11,15},{16,20},{17,... | collective-permute-start | bytes 393224 | tf_op jit(solution)/shard_map/while/body/eval_jaxpr/ppermute | solution.py:18
  84.8 2.5 %collective-permute-done.1 = bf16[64,1024]{1,0:T(8,128)(2,1)S(1)} collective-permute-done((bf16[64,1024]{1,0:T(8,128)(2,1)S(1)}, bf16[64,1024]{1,0:T(8,128)(2,1)S(1)}, u32[]{:S(2)}, u32[]{:S(2)}) %collective-permute-start.1) | collective-permute-done | bytes 131104 | tf_op jit(solution)/shard_map/while/body/eval_jaxpr/ppermute | solution.py:18
  87.3 1.3 collective-permute-start
  88.6 15.1 %all_gather.14 = bf16[64,4096]{1,0:T(8,128)(2,1)S(1)} all-gather(bf16[64,1024]{1,0:T(8,128)(2,1)S(1)} %bitcast_select_fusion.2), channel_id=1, replica_groups=mesh['dp'=4,'section'=2,'mp'=4] {'mp'}, dimensions={1}, use_global_device_ids=true | all-gather | bytes 655360 | tf_op jit(solution)/shard_map/while/body/eval_jaxpr/all_gather | solution.py:57
  103.9 6.8 %fusion.46 = bf16[64,1536]{1,0:T(8,128)(2,1)S(1)} fusion(bf16[4096,1536]{1,0:T(8,128)(2,1)} %get-tuple-element.264, bf16[64,4096]{1,0:T(8,128)(2,1)S(1)} %all_gather.14, f32[4096]{0:T(1024)S(1)} %convert_element_type.84, f32[64]{0:T(128)S(1)} %add_rsqrt_fusion.2), kind=kOutput, calls=%fused_computation.2.clone.1 | convolution fusion | flops 806289408 | bytes 13320448 | tf_op jit(solution)/shard_map/while/body/eval_jaxpr/dot_general | solution.py:61
  111.7 14.9 %all_gather.15 = bf16[64,2048]{0,1:T(8,128)(2,1)S(1)} all-gather(bf16[64,512]{0,1:T(8,128)(2,1)S(1)} %bitcast.64), channel_id=1, replica_groups=mesh['dp'=4,'section'=2,'mp'=4] {'mp'}, dimensions={1}, use_global_device_ids=true | all-gather | bytes 327680 | tf_op jit(solution)/shard_map/while/body/eval_jaxpr/all_gather | solution.py:85
  126.7 3.1 %fusion.50 = (bf16[2,64,1024]{2,1,0:T(8,128)(2,1)S(1)}, bf16[64,1024]{1,0:T(8,128)(2,1)S(1)}) fusion(bf16[2,64,1024]{2,1,0:T(8,128)(2,1)S(1)} %collective-permute-done, pred[]{:T(512)} %get-tuple-element.261, bf16[64,2048]{0,1:T(8,128)(2,1)S(1)} %all_gather.15, bf16[2048,1024]{1,0:T(8,128)(2,1)} %get-tuple-element.266, ...), kind=kOutput, calls=%fused_computation.19.clone.1 | convolution fusion | flops 268697600 | bytes 5242881 | tf_op jit(solution)/shard_map/while/body/eval_jaxpr/dot_general | solution.py:84
  129.7 4.6 %collective-permute-start.1 = (bf16[64,1024]{1,0:T(8,128)(2,1)S(1)}, bf16[64,1024]{1,0:T(8,128)(2,1)S(1)}, u32[]{:S(2)}, u32[]{:S(2)}) collective-permute-start(bf16[64,1024]{1,0:T(8,128)(2,1)S(1)} %get-tuple-element.237), channel_id=1, source_target_pairs={{0,4},{1,5},{2,6},{3,7},{8,12},{9,13},{10,14},{11,15},{16,20},{17,... | collective-permute-start | bytes 393224 | tf_op jit(solution)/shard_map/while/body/eval_jaxpr/ppermute | solution.py:18
  134.3 2.5 %collective-permute-done.1 = bf16[64,1024]{1,0:T(8,128)(2,1)S(1)} collective-permute-done((bf16[64,1024]{1,0:T(8,128)(2,1)S(1)}, bf16[64,1024]{1,0:T(8,128)(2,1)S(1)}, u32[]{:S(2)}, u32[]{:S(2)}) %collective-permute-start.1) | collective-permute-done | bytes 131104 | tf_op jit(solution)/shard_map/while/body/eval_jaxpr/ppermute | solution.py:18
  136.8 1.3 collective-permute-start
  138.1 15.3 %all_gather.14 = bf16[64,4096]{1,0:T(8,128)(2,1)S(1)} all-gather(bf16[64,1024]{1,0:T(8,128)(2,1)S(1)} %bitcast_select_fusion.2), channel_id=1, replica_groups=mesh['dp'=4,'section'=2,'mp'=4] {'mp'}, dimensions={1}, use_global_device_ids=true | all-gather | bytes 655360 | tf_op jit(solution)/shard_map/while/body/eval_jaxpr/all_gather | solution.py:57
  153.7 6.8 %fusion.46 = bf16[64,1536]{1,0:T(8,128)(2,1)S(1)} fusion(bf16[4096,1536]{1,0:T(8,128)(2,1)} %get-tuple-element.264, bf16[64,4096]{1,0:T(8,128)(2,1)S(1)} %all_gather.14, f32[4096]{0:T(1024)S(1)} %convert_element_type.84, f32[64]{0:T(128)S(1)} %add_rsqrt_fusion.2), kind=kOutput, calls=%fused_computation.2.clone.1 | convolution fusion | flops 806289408 | bytes 13320448 | tf_op jit(solution)/shard_map/while/body/eval_jaxpr/dot_general | solution.py:61
  161.5 14.8 %all_gather.15 = bf16[64,2048]{0,1:T(8,128)(2,1)S(1)} all-gather(bf16[64,512]{0,1:T(8,128)(2,1)S(1)} %bitcast.64), channel_id=1, replica_groups=mesh['dp'=4,'section'=2,'mp'=4] {'mp'}, dimensions={1}, use_global_device_ids=true | all-gather | bytes 327680 | tf_op jit(solution)/shard_map/while/body/eval_jaxpr/all_gather | solution.py:85
  176.3 3.1 %fusion.50 = (bf16[2,64,1024]{2,1,0:T(8,128)(2,1)S(1)}, bf16[64,1024]{1,0:T(8,128)(2,1)S(1)}) fusion(bf16[2,64,1024]{2,1,0:T(8,128)(2,1)S(1)} %collective-permute-done, pred[]{:T(512)} %get-tuple-element.261, bf16[64,2048]{0,1:T(8,128)(2,1)S(1)} %all_gather.15, bf16[2048,1024]{1,0:T(8,128)(2,1)} %get-tuple-element.266, ...), kind=kOutput, calls=%fused_computation.19.clone.1 | convolution fusion | flops 268697600 | bytes 5242881 | tf_op jit(solution)/shard_map/while/body/eval_jaxpr/dot_general | solution.py:84
  179.3 4.7 %collective-permute-start.1 = (bf16[64,1024]{1,0:T(8,128)(2,1)S(1)}, bf16[64,1024]{1,0:T(8,128)(2,1)S(1)}, u32[]{:S(2)}, u32[]{:S(2)}) collective-permute-start(bf16[64,1024]{1,0:T(8,128)(2,1)S(1)} %get-tuple-element.237), channel_id=1, source_target_pairs={{0,4},{1,5},{2,6},{3,7},{8,12},{9,13},{10,14},{11,15},{16,20},{17,... | collective-permute-start | bytes 393224 | tf_op jit(solution)/shard_map/while/body/eval_jaxpr/ppermute | solution.py:18
  184.0 2.5 %collective-permute-done.1 = bf16[64,1024]{1,0:T(8,128)(2,1)S(1)} collective-permute-done((bf16[64,1024]{1,0:T(8,128)(2,1)S(1)}, bf16[64,1024]{1,0:T(8,128)(2,1)S(1)}, u32[]{:S(2)}, u32[]{:S(2)}) %collective-permute-start.1) | collective-permute-done | bytes 131104 | tf_op jit(solution)/shard_map/while/body/eval_jaxpr/ppermute | solution.py:18
  (50 shorter events, 5.0 us)
Async XLA Ops:
  0.0 33.6 %copy-start = (f32[8,32]{1,0:T(8,128)S(1)}, f32[8,32]{1,0:T(8,128)}, u32[]{:S(2)}) copy-start(f32[8,32]{1,0:T(8,128)} %param.14) | copy-start | bytes 3076
  17.0 16.7 %copy-start.2 = (s32[64,64]{1,0:T(8,128)S(1)}, s32[64,64]{1,0:T(8,128)}, u32[]{:S(2)}) copy-start(s32[64,64]{1,0:T(8,128)} %constant.94.clone) | copy-start | bytes 49156
  17.0 17.2 %copy-start.1 = (bf16[1,64,1024]{2,1,0:T(8,128)(2,1)S(1)}, bf16[1,64,1024]{2,1,0:T(8,128)(2,1)}, u32[]{:S(2)}) copy-start(bf16[1,64,1024]{2,1,0:T(8,128)(2,1)} %param.10) | copy-start | bytes 393220
  17.0 17.3 %copy-start.3 = (bf16[1,4096]{1,0:T(2,128)(2,1)S(1)}, bf16[1,4096]{1,0:T(2,128)(2,1)}, u32[]{:S(2)}) copy-start(bf16[1,4096]{1,0:T(2,128)(2,1)} %param.13) | copy-start | bytes 24580
  34.4 43.0 %collective-permute-start = (bf16[2,64,1024]{2,1,0:T(8,128)(2,1)S(1)}, bf16[2,64,1024]{2,1,0:T(8,128)(2,1)S(1)}, u32[]{:S(2)}, u32[]{:S(2)}) collective-permute-start(bf16[2,64,1024]{2,1,0:T(8,128)(2,1)S(1)} %get-tuple-element.249), channel_id=1, source_target_pairs={{4,0},{5,1},{6,2},{7,3},{12,8},{13,9},{14,10},{15,11},{20,16},{21,... | collective-permute-start | bytes 786440 | tf_op jit(solution)/shard_map/while/body/eval_jaxpr/ppermute | solution.py:18
  80.4 6.8 %collective-permute-start.1 = (bf16[64,1024]{1,0:T(8,128)(2,1)S(1)}, bf16[64,1024]{1,0:T(8,128)(2,1)S(1)}, u32[]{:S(2)}, u32[]{:S(2)}) collective-permute-start(bf16[64,1024]{1,0:T(8,128)(2,1)S(1)} %get-tuple-element.237), channel_id=1, source_target_pairs={{0,4},{1,5},{2,6},{3,7},{8,12},{9,13},{10,14},{11,15},{16,20},{17,... | collective-permute-start | bytes 393224 | tf_op jit(solution)/shard_map/while/body/eval_jaxpr/ppermute | solution.py:18
  87.3 39.4 %collective-permute-start = (bf16[2,64,1024]{2,1,0:T(8,128)(2,1)S(1)}, bf16[2,64,1024]{2,1,0:T(8,128)(2,1)S(1)}, u32[]{:S(2)}, u32[]{:S(2)}) collective-permute-start(bf16[2,64,1024]{2,1,0:T(8,128)(2,1)S(1)} %get-tuple-element.249), channel_id=1, source_target_pairs={{4,0},{5,1},{6,2},{7,3},{12,8},{13,9},{14,10},{15,11},{20,16},{21,... | collective-permute-start | bytes 786440 | tf_op jit(solution)/shard_map/while/body/eval_jaxpr/ppermute | solution.py:18
  129.7 7.1 %collective-permute-start.1 = (bf16[64,1024]{1,0:T(8,128)(2,1)S(1)}, bf16[64,1024]{1,0:T(8,128)(2,1)S(1)}, u32[]{:S(2)}, u32[]{:S(2)}) collective-permute-start(bf16[64,1024]{1,0:T(8,128)(2,1)S(1)} %get-tuple-element.237), channel_id=1, source_target_pairs={{0,4},{1,5},{2,6},{3,7},{8,12},{9,13},{10,14},{11,15},{16,20},{17,... | collective-permute-start | bytes 393224 | tf_op jit(solution)/shard_map/while/body/eval_jaxpr/ppermute | solution.py:18
  136.8 39.5 %collective-permute-start = (bf16[2,64,1024]{2,1,0:T(8,128)(2,1)S(1)}, bf16[2,64,1024]{2,1,0:T(8,128)(2,1)S(1)}, u32[]{:S(2)}, u32[]{:S(2)}) collective-permute-start(bf16[2,64,1024]{2,1,0:T(8,128)(2,1)S(1)} %get-tuple-element.249), channel_id=1, source_target_pairs={{4,0},{5,1},{6,2},{7,3},{12,8},{13,9},{14,10},{15,11},{20,16},{21,... | collective-permute-start | bytes 786440 | tf_op jit(solution)/shard_map/while/body/eval_jaxpr/ppermute | solution.py:18
  179.3 7.2 %collective-permute-start.1 = (bf16[64,1024]{1,0:T(8,128)(2,1)S(1)}, bf16[64,1024]{1,0:T(8,128)(2,1)S(1)}, u32[]{:S(2)}, u32[]{:S(2)}) collective-permute-start(bf16[64,1024]{1,0:T(8,128)(2,1)S(1)} %get-tuple-element.237), channel_id=1, source_target_pairs={{0,4},{1,5},{2,6},{3,7},{8,12},{9,13},{10,14},{11,15},{16,20},{17,... | collective-permute-start | bytes 393224 | tf_op jit(solution)/shard_map/while/body/eval_jaxpr/ppermute | solution.py:18
where the time goes:
time: 188 us; the launch traced here: 187 us
  blocking collectives  93.7 us (50%)
  local copies, waits for them, and re-layouts  35.9 us (19%)
  matrix products  31.3 us (17%)
  starting transfers between devices  17.4 us (9%)
  waiting for transfers between devices  7.42 us (4%)
    all_gather x3, blocking collectives, attend(): lax.all_gather(section_in, 'mp', axis=1, tiled=True).astype(jnp.float32)  47.8 us
    all_gather x3, blocking collectives, attend(): lax.all_gather(head_mix, 'mp', axis=1, tiled=True)  46 us
    dot_general x3, matrix products, attend(): jnp.dot(gained_piece, weight_block, preferred_element_type=jnp.float32)  20.5 us
    ppermute x6, starting transfers between devices, shifted(): return lax.ppermute(x, axis, pairs)  17.4 us
    unnamed x9, local copies, waits for them, and re-layouts  17 us
    while x2, local copies, waits for them, and re-layouts, shards(): final_pair = lax.fori_loop(0, ticks, conveyor_tick, (belt_start, blank))  16.8 us
    dot_general x3, matrix products, attend(): jnp.dot(lax.all_gather(head_mix, 'mp', axis=1, tiled=True), weight_block,...  9.19 us
    ppermute x6, waiting for transfers between devices, shifted(): return lax.ppermute(x, axis, pairs)  7.42 us
  transfers between devices with their start and end apart: 6, of which 3 were waited for; matrix products, arithmetic and copies ran while one was open for 13% of the time, Pallas kernels for 0%

commit v1 on v0

v1 whole, which is shorter than its diff:
```python
import functools
import math

import jax
import jax.numpy as jnp
import numpy as np
from jax import lax
from jax.experimental import pallas as pl
from jax.experimental.pallas import tpu as pltpu
from jax.sharding import PartitionSpec as P

REACH = 128
NORM_EPSILON = 0.1
MESH = pl.DeviceIdType.MESH


def bucket_table(length, bucket_count, reach_limit):
    offset = np.arange(length)[None, :] - np.arange(length)[:, None]
    half_count = bucket_count // 2
    upper_side = (offset > 0).astype(np.int32) * half_count
    distance = np.abs(offset)
    exact_count = half_count // 2
    scaled = (
        np.log(np.maximum(distance, 1) / exact_count)
        / np.log(reach_limit / exact_count)
        * (half_count - exact_count)
    )
    far_bucket = np.minimum(exact_count + scaled.astype(np.int32), half_count - 1)
    return (upper_side + np.where(distance < exact_count, distance, far_bucket)).astype(np.int32)


def relay_chunks(rows):
    units = rows // 16
    here = max(1, (3 * units) // 8)
    there = units - here
    first = (there + 1) // 2
    cuts = [(0, first * 16), (first * 16, (there - first) * 16)]
    return [c for c in cuts if c[1]], (there * 16, here * 16)


def kernel(
    sizes,
    x_ref, gain_ref, bucket_ref, pbias_ref, wq_hbm, wo_hbm,
    o_ref,
    pre, xg, hg, spread, ho, fin, wq, wo, acc, acc2, sq, qkv, bias,
    wq_sem, wo_sem,
    pre_recv, pre_send, pre_up, in_recv,
    hop_send, hop_recv, hop_line,
    spread_recv, spread_send, spread_up, late_recv,
    mix_recv, mix_send,
    fin_send, fin_recv,
):
    S, M, L, H, hs = sizes
    Dl = x_ref.shape[1]
    Wl = H * hs
    R = S * L
    D = M * Dl
    s = lax.axis_index("section")
    m = lax.axis_index("mp")
    hops, (late_at, late_rows) = relay_chunks(R)
    late = pl.ds(late_at, late_rows)

    def to(src, dst, send, recv, sec, col):
        return pltpu.make_async_remote_copy(
            src_ref=src, dst_ref=dst, send_sem=send, recv_sem=recv,
            device_id={"section": sec, "mp": col}, device_id_type=MESH,
        )

    def along(j, src, dst, send, recv, act):
        @pl.when((j <= m) & (m < M - 1))
        def _():
            act(to(src, dst, send.at[0, j], recv, s, m + 1))

        @pl.when((j >= m) & (m > 0))
        def _():
            act(to(src, dst, send.at[1, j], recv, s, m - 1))

    def start(c):
        c.start()

    def sent(c):
        c.wait_send()

    def got(dst, recv):
        to(dst, dst, fin_send.at[0], recv, s, lax.rem(m + 1, M)).wait_recv()

    near = jnp.minimum(m, M - 1 - m)
    longer = jnp.where(m > M - 1 - m, -1, 1)

    def nth(p):
        k = (p + 1) // 2
        both = jnp.where(p % 2 == 1, -k, k)
        return m + jnp.where(p <= 2 * near, both, longer * (p - near))

    def wq_copy(j):
        rows = pl.ds(pl.multiple_of(j * Dl, Dl), Dl)
        return pltpu.make_async_copy(wq_hbm.at[:, rows, :], wq.at[:, rows, :], wq_sem.at[j])

    def wo_copy():
        return pltpu.make_async_copy(wo_hbm, wo, wo_sem)

    for p in range(M):
        wq_copy(nth(p)).start()
    wo_copy().start()

    barrier = pltpu.get_barrier_semaphore()

    @pl.when(m > 0)
    def _():
        pl.semaphore_signal(barrier, inc=1, device_id={"section": s, "mp": m - 1}, device_id_type=MESH)

    @pl.when(m < M - 1)
    def _():
        pl.semaphore_signal(barrier, inc=1, device_id={"section": s, "mp": m + 1}, device_id_type=MESH)

    for k in range(1, S):
        pl.semaphore_signal(
            barrier, inc=1, device_id={"section": lax.rem(s + k, S), "mp": m}, device_id_type=MESH
        )
    pl.semaphore_wait(
        barrier, S - 1 + jnp.where(m > 0, 1, 0) + jnp.where(m < M - 1, 1, 0)
    )

    def up_rows(j):
        return xg.at[j, pl.ds(pl.multiple_of(s * L, L), L), :]

    def first_act(act):
        along(m, x_ref, pre.at[m], pre_send, pre_recv.at[m], act)

        @pl.when(s > 0)
        def _():
            act(to(x_ref, up_rows(m), pre_up.at[m], in_recv.at[s, m], 0, m))

    def pre_act(j, act):
        along(j, pre.at[j], pre.at[j], pre_send, pre_recv.at[j], act)

        @pl.when(s > 0)
        def _():
            act(to(pre.at[j], up_rows(j), pre_up.at[j], in_recv.at[s, j], 0, m))

    first_act(start)

    @pl.when(s == 0)
    def _():
        xg[m, 0:L, :] = x_ref[...]

    for h in range(H):
        total = jnp.zeros(bucket_ref.shape, jnp.float32)
        for b in range(pbias_ref.shape[1]):
            total = jnp.where(bucket_ref[...] == b, pbias_ref[h, b], total)
        bias[h] = total
    acc[...] = jnp.zeros_like(acc)
    acc2[...] = jnp.zeros_like(acc2)
    sq[...] = jnp.zeros_like(sq)

    def pre_step(p, carry):
        j = nth(p)
        got(pre.at[j], pre_recv.at[j])
        pre_act(j, start)

        @pl.when(s == 0)
        def _():
            xg[j, 0:L, :] = pre[j]

        return carry

    lax.fori_loop(1, M, pre_step, 0)

    def hop_act(c, j, act):
        at, rows = hops[c]
        block = xg.at[j, pl.ds(at, rows), :]
        along(j, block, block, hop_line.at[c], hop_recv.at[c, j], act)

    def qkv_step(p, carry):
        j = nth(p)

        @pl.when(s == 0)
        def _():
            for o in range(1, S):
                got(xg.at[j, pl.ds(o * L, L), :], in_recv.at[o, j])

        @pl.when(s > 0)
        def _():
            for c, (at, rows) in enumerate(hops):
                got(xg.at[j, pl.ds(at, rows), :], hop_recv.at[c, j])
                hop_act(c, j, start)
            got(xg.at[j, late, :], late_recv.at[j])

        wq_copy(j).wait()
        block = xg[j].astype(jnp.float32)
        squares = block * block
        part = squares[:, 0:128]
        for k in range(1, Dl // 128):
            part = part + squares[:, k * 128 : (k + 1) * 128]
        sq[...] += part
        gained = (block * gain_ref[j]).astype(jnp.bfloat16)
        rows = pl.ds(pl.multiple_of(j * Dl, Dl), Dl)
        for t in range(3):
            cols = pl.ds(t * Wl, Wl)
            acc[:, cols] += jnp.dot(gained, wq[t, rows, :], preferred_element_type=jnp.float32)
        return carry

    lax.fori_loop(0, M, qkv_step, 0)
    row_scale = lax.rsqrt(jnp.sum(sq[...], axis=1, keepdims=True) / D + NORM_EPSILON)
    qkv[...] = (acc[...] * row_scale).astype(jnp.bfloat16)

    mix_rows = L * ((S + 1) // 2)
    mixes = [(at, min(mix_rows, R - at)) for at in range(0, R, mix_rows)]

    def mix_act(c, j, act):
        at, rows = mixes[c]
        block = hg.at[j, pl.ds(at, rows), :]
        along(j, block, block, mix_send.at[c], mix_recv.at[c, j], act)

    scale = 1.0 / math.sqrt(hs)

    def attend(at):
        rows = pl.ds(at, L)
        outs = []
        for h in range(H):
            q = qkv[rows, h * hs : (h + 1) * hs]
            k = qkv[rows, Wl + h * hs : Wl + (h + 1) * hs]
            v = qkv[rows, 2 * Wl + h * hs : 2 * Wl + (h + 1) * hs]
            scores = lax.dot_general(
                q, k, (((1,), (1,)), ((), ())), preferred_element_type=jnp.float32
            ) * scale + bias[h]
            weights = jnp.exp(scores - jnp.max(scores, axis=1, keepdims=True))
            probs = (weights / jnp.sum(weights, axis=1, keepdims=True)).astype(jnp.bfloat16)
            outs.append(jnp.dot(probs, v, preferred_element_type=jnp.float32).astype(jnp.bfloat16))
        hg[m, rows, :] = jnp.concatenate(outs, axis=1)

    for c, (at, rows) in enumerate(mixes):
        if rows == L:
            attend(at)
        else:
            def attend_step(i, carry):
                attend(pl.multiple_of(at + i * L, L))
                return carry

            lax.fori_loop(0, rows // L, attend_step, 0)
        mix_act(c, m, start)

    wo_copy().wait()

    def project(j):
        rows = pl.ds(pl.multiple_of(j * Wl, Wl), Wl)
        acc2[...] += jnp.dot(hg[j], wo[rows, :], preferred_element_type=jnp.float32)

    project(m)

    def mix_step(p, carry):
        j = nth(p)
        for c, (at, rows) in enumerate(mixes):
            got(hg.at[j, pl.ds(at, rows), :], mix_recv.at[c, j])
            mix_act(c, j, start)
        project(j)
        return carry

    lax.fori_loop(1, M, mix_step, 0)
    ho[...] = (xg[m].astype(jnp.float32) + acc2[...]).astype(jnp.bfloat16)

    own_late = ho.at[late, :]

    def hop_out(act):
        for c, (at, rows) in enumerate(hops):
            act(to(ho.at[pl.ds(at, rows), :], xg.at[m, pl.ds(at, rows), :],
                   hop_send.at[c], hop_recv.at[c, m], s + 1, m))

    def late_out(j, src, act):
        along(j, src, spread.at[j], spread_send, spread_recv.at[j], act)
        act(to(src, xg.at[j, late, :], spread_up.at[j], late_recv.at[j], s + 1, m))

    def home(act):
        for o in range(S - 1):
            act(to(ho.at[pl.ds(o * L, L), :], fin, fin_send.at[o], fin_recv, o, m))

    @pl.when(s < S - 1)
    def _():
        hop_out(start)
        late_out(m, own_late, start)

        def late_step(p, carry):
            j = nth(p)
            got(spread.at[j], spread_recv.at[j])
            late_out(j, spread.at[j], start)
            return carry

        lax.fori_loop(1, M, late_step, 0)

    @pl.when(s == S - 1)
    def _():
        home(start)
        o_ref[...] = ho[(S - 1) * L :, :]

    first_act(sent)
    for c in range(len(mixes)):
        mix_act(c, m, sent)

    @pl.when(s > 0)
    def _():
        for c in range(len(hops)):
            hop_act(c, m, sent)

    @pl.when(s < S - 1)
    def _():
        hop_out(sent)
        late_out(m, own_late, sent)

    def drain_step(p, carry):
        j = nth(p)
        pre_act(j, sent)
        for c in range(len(mixes)):
            mix_act(c, j, sent)

        @pl.when(s > 0)
        def _():
            for c in range(len(hops)):
                hop_act(c, j, sent)

        @pl.when(s < S - 1)
        def _():
            late_out(j, spread.at[j], sent)

        return carry

    lax.fori_loop(1, M, drain_step, 0)

    @pl.when(s == S - 1)
    def _():
        home(sent)

    @pl.when(s < S - 1)
    def _():
        got(fin, fin_recv)
        o_ref[...] = fin[...]


def solution(mesh):
    S, M = mesh.shape["section"], mesh.shape["mp"]

    def shards(micro_inputs, qkv_weight, out_weight, norm_gain, position_bias):
        L, Dl = micro_inputs.shape[1:]
        D = qkv_weight.shape[1]
        Wl = qkv_weight.shape[3]
        H = position_bias.shape[0]
        R = S * L
        hops, (_, late_rows) = relay_chunks(R)
        mixes = -(-R // (L * ((S + 1) // 2)))
        buckets = jnp.asarray(bucket_table(L, position_bias.shape[1], REACH))
        gain = norm_gain.reshape(M, 1, Dl).astype(jnp.float32)
        wq = jnp.transpose(qkv_weight[0], (1, 0, 2))
        bf16, f32 = jnp.bfloat16, jnp.float32
        dma = pltpu.SemaphoreType.DMA
        vmem = pl.BlockSpec(memory_space=pltpu.VMEM)
        out = pl.pallas_call(
            functools.partial(kernel, (S, M, L, H, Wl // H)),
            out_shape=jax.ShapeDtypeStruct((L, Dl), bf16),
            in_specs=[
                vmem, vmem, vmem, pl.BlockSpec(memory_space=pltpu.SMEM),
                pl.BlockSpec(memory_space=pl.ANY), pl.BlockSpec(memory_space=pl.ANY),
            ],
            out_specs=vmem,
            scratch_shapes=[
                pltpu.VMEM((M, L, Dl), bf16),
                pltpu.VMEM((M, R, Dl), bf16),
                pltpu.VMEM((M, R, Wl), bf16),
                pltpu.VMEM((M, late_rows, Dl), bf16),
                pltpu.VMEM((R, Dl), bf16),
                pltpu.VMEM((L, Dl), bf16),
                pltpu.VMEM((3, D, Wl), bf16),
                pltpu.VMEM((M * Wl, Dl), bf16),
                pltpu.VMEM((R, 3 * Wl), f32),
                pltpu.VMEM((R, Dl), f32),
                pltpu.VMEM((R, 128), f32),
                pltpu.VMEM((R, 3 * Wl), bf16),
                pltpu.VMEM((H, L, L), f32),
                dma((M,)), dma,
                dma((M,)), dma((2, M)), dma((M,)), dma((S, M)),
                dma((len(hops),)), dma((len(hops), M)), dma((len(hops), 2, M)),
                dma((M,)), dma((2, M)), dma((M,)), dma((M,)),
                dma((mixes, M)), dma((mixes, 2, M)),
                dma((S,)), dma,
            ],
            compiler_params=pltpu.CompilerParams(
                collective_id=0, has_side_effects=True, vmem_limit_bytes=60 * 1024 * 1024
            ),
        )(micro_inputs[0], gain, buckets, position_bias, wq, out_weight[0])
        return out[None]

    in_specs = (
        P(("dp", "section"), None, "mp"),
        P("section", None, None, "mp"),
        P("section", None, "mp"),
        P("section", None),
        P("mp", None),
    )
    out_specs = P(("dp", "section"), None, "mp")
    return jax.shard_map(shards, mesh=mesh, in_specs=in_specs, out_specs=out_specs, check_vma=False)
```

time: 188 us -> 80.1 us (0.43)
  blocking collectives: 93.7 us -> 0 us
  Pallas kernels: 0 us -> 77 us
  local copies, waits for them, and re-layouts: 35.9 us -> 1.57 us
  matrix products: 31.3 us -> 0 us
  starting transfers between devices: 17.4 us -> 0 us
  waiting for transfers between devices: 7.42 us -> 0 us
    all_gather x6 -> x0, blocking collectives: 93.7 us -> none  [the longest x3 47.8 us: attend(): lax.all_gather(section_in, 'mp', axis=1, tiled=True).astype(jnp.float32)]
    pallas_call x0 -> x1, Pallas kernels: none -> 77 us  [shards(): pl.pallas_call(functools.partial(kernel, (S, M, L, H, Wl // H)), out_shap...]
    dot_general x13 -> x0, matrix products: 31.3 us -> none  [the longest x3 20.5 us: attend(): jnp.dot(gained_piece, weight_block, preferred_element_type=jnp.float32)]
    ppermute x6 -> x0, starting transfers between devices: 17.4 us -> none  [shifted(): return lax.ppermute(x, axis, pairs)]
    while x8 -> x0, local copies, waits for them, and re-layouts: 17.3 us -> none  [the longest x2 16.8 us: shards(): final_pair = lax.fori_loop(0, ticks, conveyor_tick, (belt_start, blank))]
    unnamed x9 -> x1, local copies, waits for them, and re-layouts: 17 us -> 1.57 us
    ppermute x6 -> x0, waiting for transfers between devices: 7.42 us -> none  [shifted(): return lax.ppermute(x, axis, pairs)]
  transfers between devices with their start and end apart: 6 -> 0, of which waited for: 3 -> 0; matrix products, arithmetic and copies ran while one was open for 13% -> 0% of each run, Pallas kernels for 0% -> 0%
where the time goes in v1:
time: 80.1 us; the launch traced here: 79.9 us
  Pallas kernels  77 us (96%)
  local copies, waits for them, and re-layouts  1.57 us (2%)
  other arithmetic  1.34 us (2%)
    pallas_call x1, Pallas kernels, shards(): pl.pallas_call(functools.partial(kernel, (S, M, L, H, Wl // H)), out_shap...  77 us

profile of v1, /device:TPU:0, one launch (start us, length us, event | category | flops | bytes accessed | tf_op | source)
XLA Modules:
  0.0 79.9 jit_solution(8918738757711945641)
XLA Ops:
  0.0 1.3 %convert.1.gain_ref = f32[4,1,1024]{2,1,0:T(1,128)} convert(bf16[4,1,1024]{2,1,0:T(2,128)(2,1)} %bitcast.12) | non-fusion elementwise | flops 4096 | bytes 24576 | tf_op jit(solution)/shard_map/convert_element_type | solution.py:350
  1.3 77.0 %shard_map.64 = bf16[64,1024]{1,0:T(8,128)(2,1)} custom-call(bf16[64,1024]{1,0:T(8,128)(2,1)} %bitcast.11, f32[4,1,1024]{2,1,0:T(1,128)} %convert.1.gain_ref, s32[64,64]{1,0:T(8,128)} %constant.2.clone.bucket_ref, f32[8,32]{1,0:T(8,128)} %pbias_ref.1, bf16[3,4096,512]{2,1,0:T(8,128)(2,1)} %bitcast.8, bf16[2048,1024]{1,0:T(8,128)(2,1)} %bitcast.9), custom_call_target="tpu_custom_call" | custom-call | tf_op jit(solution)/shard_map/pallas_call | solution.py:355
  78.3 1.6 %copy.8 = bf16[1,64,1024]{2,1,0:T(8,128)(2,1)} copy(bf16[1,64,1024]{2,1,0:T(8,128)(2,1)} %bitcast.10) | data formatting | bytes 262144

commit v2 on v1

v2 whole, which is shorter than its diff:
```python
import functools
import math

import jax
import jax.numpy as jnp
import numpy as np
from jax import lax
from jax.experimental import pallas as pl
from jax.experimental.pallas import tpu as pltpu
from jax.sharding import PartitionSpec as P

REACH = 128
NORM_EPSILON = 0.1
MESH = pl.DeviceIdType.MESH


def bucket_table(length, bucket_count, reach_limit):
    offset = np.arange(length)[None, :] - np.arange(length)[:, None]
    half_count = bucket_count // 2
    upper_side = (offset > 0).astype(np.int32) * half_count
    distance = np.abs(offset)
    exact_count = half_count // 2
    scaled = (
        np.log(np.maximum(distance, 1) / exact_count)
        / np.log(reach_limit / exact_count)
        * (half_count - exact_count)
    )
    far_bucket = np.minimum(exact_count + scaled.astype(np.int32), half_count - 1)
    return (upper_side + np.where(distance < exact_count, distance, far_bucket)).astype(np.int32)


def relay_chunks(micro, micros, length):
    here = length // 2 // 16 * 16 if micro == micros - 1 else 0
    there = length - here
    half = max(16, there // 2 // 16 * 16)
    return [(at, min(half, there - at)) for at in range(0, there, half)], (there, here)


def head_group(heads, head_size):
    return max(g for g in range(1, heads + 1) if heads % g == 0 and g * head_size <= 256)


def kernel(
    sizes,
    x_ref, gain_ref, bucket_ref, pbias_ref, wq_hbm, wo_hbm,
    o_ref,
    pre, xg, hg, spread, ho, fin, wq, wo, acc, sq, qkv, bias, head_mask,
    wq_sem, wo_sem,
    pre_recv, pre_send, pre_up, in_recv,
    hop_send, hop_recv, hop_line,
    spread_recv, spread_send, spread_up, late_recv,
    mix_recv, mix_send,
    fin_send, fin_recv,
):
    S, M, L, H, hs = sizes
    Dl = x_ref.shape[1]
    Wl = H * hs
    G = head_group(H, hs)
    Wg = G * hs
    D = M * Dl
    s = lax.axis_index("section")
    m = lax.axis_index("mp")
    plans = [relay_chunks(i, S, L) for i in range(S)]

    def to(src, dst, send, recv, sec, col):
        return pltpu.make_async_remote_copy(
            src_ref=src, dst_ref=dst, send_sem=send, recv_sem=recv,
            device_id={"section": sec, "mp": col}, device_id_type=MESH,
        )

    def along(j, src, dst, send, recv, act):
        @pl.when((j <= m) & (m < M - 1))
        def _():
            act(to(src, dst, send.at[0, j], recv, s, m + 1))

        @pl.when((j >= m) & (m > 0))
        def _():
            act(to(src, dst, send.at[1, j], recv, s, m - 1))

    def start(c):
        c.start()

    def sent(c):
        c.wait_send()

    def got(dst, recv):
        to(dst, dst, fin_send.at[0], recv, s, lax.rem(m + 1, M)).wait_recv()

    near = jnp.minimum(m, M - 1 - m)
    longer = jnp.where(m > M - 1 - m, -1, 1)

    def nth(p):
        k = (p + 1) // 2
        both = jnp.where(p % 2 == 1, -k, k)
        return m + jnp.where(p <= 2 * near, both, longer * (p - near))

    def wq_copy(j):
        rows = pl.ds(pl.multiple_of(j * Dl, Dl), Dl)
        return pltpu.make_async_copy(wq_hbm.at[:, rows, :], wq.at[:, rows, :], wq_sem.at[j])

    def wo_copy():
        return pltpu.make_async_copy(wo_hbm, wo, wo_sem)

    barrier = pltpu.get_barrier_semaphore()
    for k in range(1, M):
        pl.semaphore_signal(
            barrier, inc=1, device_id={"section": s, "mp": lax.rem(m + k, M)}, device_id_type=MESH
        )
    for k in range(1, S):
        pl.semaphore_signal(
            barrier, inc=1, device_id={"section": lax.rem(s + k, S), "mp": m}, device_id_type=MESH
        )

    for p in range(M):
        wq_copy(nth(p)).start()
    wo_copy().start()
    pl.semaphore_wait(barrier, S + M - 2)

    def up_rows(j):
        return xg.at[j, pl.ds(pl.multiple_of(s * L, L), L), :]

    def first_act(act):
        along(m, x_ref, pre.at[m], pre_send, pre_recv.at[m], act)

        @pl.when(s > 0)
        def _():
            act(to(x_ref, up_rows(m), pre_up.at[m], in_recv.at[s, m], 0, m))

    def pre_act(j, act):
        along(j, pre.at[j], pre.at[j], pre_send, pre_recv.at[j], act)

        @pl.when(s > 0)
        def _():
            act(to(pre.at[j], up_rows(j), pre_up.at[j], in_recv.at[s, j], 0, m))

    first_act(start)

    for g in range(H // G):
        heads = []
        for h in range(g * G, (g + 1) * G):
            total = jnp.zeros(bucket_ref.shape, jnp.float32)
            for b in range(pbias_ref.shape[1]):
                total = jnp.where(bucket_ref[...] == b, pbias_ref[h, b], total)
            heads.append(total)
        bias[g] = jnp.concatenate(heads, axis=1)
    head_mask[...] = jnp.where(
        lax.broadcasted_iota(jnp.int32, (G * L, Wg), 0) // L
        == lax.broadcasted_iota(jnp.int32, (G * L, Wg), 1) // hs,
        1.0,
        0.0,
    ).astype(jnp.bfloat16)

    @pl.when(s > 0)
    def _():
        def pre_step(p, carry):
            j = nth(p)
            got(pre.at[j], pre_recv.at[j])
            pre_act(j, start)
            return carry

        lax.fori_loop(1, M, pre_step, 0)

    def hop_block(i, c, j):
        at, rows = plans[i][0][c]
        return xg.at[j, pl.ds(i * L + at, rows), :]

    def hop_act(i, c, j, act):
        block = hop_block(i, c, j)
        along(j, block, block, hop_line.at[i, c], hop_recv.at[i, c, j], act)

    def late_block(i, j):
        at, rows = plans[i][1]
        return xg.at[j, pl.ds(i * L + at, rows), :]

    def spread_block(i, j):
        return spread.at[i, j, pl.ds(0, plans[i][1][1]), :]

    def receive(i, j):
        @pl.when(s == 0)
        def _():
            if i:
                got(xg.at[j, pl.ds(i * L, L), :], in_recv.at[i, j])
            else:
                @pl.when(j == m)
                def _():
                    xg[m, 0:L, :] = x_ref[...]

                @pl.when(j != m)
                def _():
                    got(pre.at[j], pre_recv.at[j])
                    pre_act(j, start)
                    xg[j, 0:L, :] = pre[j]

        @pl.when(s > 0)
        def _():
            for c in range(len(plans[i][0])):
                got(hop_block(i, c, j), hop_recv.at[i, c, j])
                hop_act(i, c, j, start)
            if plans[i][1][1]:
                got(late_block(i, j), late_recv.at[i, j])

    def mix_act(i, act):
        block = hg.at[pl.ds(i * L, L), pl.ds(pl.multiple_of(m * Wl, Wl), Wl)]
        for k in range(1, M):
            col = lax.rem(m + k, M)
            act(to(block, block, mix_send.at[i, k], mix_recv.at[i, m], s, col))

    scale = 1.0 / math.sqrt(hs)
    lane_head = lax.broadcasted_iota(jnp.int32, (L, Wg), 1) // hs

    def attend(i):
        for g in range(H // G):
            q = qkv[:, g * Wg : (g + 1) * Wg]
            k = qkv[:, Wl + g * Wg : Wl + (g + 1) * Wg]
            v = qkv[:, 2 * Wl + g * Wg : 2 * Wl + (g + 1) * Wg]
            apart = jnp.concatenate([q] * G, axis=0) * head_mask[...]
            scores = lax.dot_general(
                k, apart, (((1,), (1,)), ((), ())), preferred_element_type=jnp.float32
            ) * scale + bias[g]
            weights = jnp.exp(scores - jnp.max(scores, axis=0, keepdims=True))
            probs = (weights / jnp.sum(weights, axis=0, keepdims=True)).astype(jnp.bfloat16)
            mixed = lax.dot_general(
                probs, v, (((0,), (0,)), ((), ())), preferred_element_type=jnp.float32
            )
            out = mixed[0:L]
            for h in range(1, G):
                out = jnp.where(lane_head == h, mixed[h * L : (h + 1) * L], out)
            cols = pl.ds(pl.multiple_of(m * Wl + g * Wg, Wg), Wg)
            hg[i * L : (i + 1) * L, cols] = out.astype(jnp.bfloat16)

    for i in range(S):
        acc[...] = jnp.zeros_like(acc)
        sq[...] = jnp.zeros_like(sq)

        def qkv_step(p, carry):
            j = nth(p)
            receive(i, j)
            if i == 0:
                wq_copy(j).wait()
            block = xg[j, i * L : (i + 1) * L, :].astype(jnp.float32)
            squares = block * block
            part = squares[:, 0:128]
            for k in range(1, Dl // 128):
                part = part + squares[:, k * 128 : (k + 1) * 128]
            sq[...] += part
            rows = pl.ds(pl.multiple_of(j * Dl, Dl), Dl)
            gained = (block * gain_ref[:, rows].astype(jnp.float32)).astype(jnp.bfloat16)
            for t in range(3):
                cols = pl.ds(t * Wl, Wl)
                acc[:, cols] += jnp.dot(gained, wq[t, rows, :], preferred_element_type=jnp.float32)
            return carry

        lax.fori_loop(0, M, qkv_step, 0)
        row_scale = lax.rsqrt(jnp.sum(sq[...], axis=1, keepdims=True) / D + NORM_EPSILON)
        qkv[...] = (acc[...] * row_scale).astype(jnp.bfloat16)
        attend(i)
        mix_act(i, start)

    wo_copy().wait()

    def hop_out(i, act):
        for c, (at, rows) in enumerate(plans[i][0]):
            act(to(ho.at[pl.ds(i * L + at, rows), :], hop_block(i, c, m),
                   hop_send.at[i, c], hop_recv.at[i, c, m], s + 1, m))

    def late_out(i, j, src, act):
        along(j, src, spread_block(i, j), spread_send.at[i], spread_recv.at[i, j], act)
        act(to(src, late_block(i, j), spread_up.at[i, j], late_recv.at[i, j], s + 1, m))

    def own_late(i):
        at, rows = plans[i][1]
        return ho.at[pl.ds(i * L + at, rows), :]

    def home(i, act):
        act(to(ho.at[pl.ds(i * L, L), :], fin, fin_send.at[i], fin_recv, i, m))

    for i in range(S):
        for k in range(1, M):
            j = lax.rem(m + k, M)
            got(hg.at[pl.ds(i * L, L), pl.ds(pl.multiple_of(j * Wl, Wl), Wl)], mix_recv.at[i, j])
        rows = slice(i * L, (i + 1) * L)
        update = jnp.dot(hg[rows, :], wo[...], preferred_element_type=jnp.float32)
        ho[rows, :] = (xg[m, rows, :].astype(jnp.float32) + update).astype(jnp.bfloat16)

        @pl.when(s < S - 1)
        def _():
            hop_out(i, start)
            if plans[i][1][1]:
                late_out(i, m, own_late(i), start)

                def late_step(p, carry):
                    j = nth(p)
                    got(spread_block(i, j), spread_recv.at[i, j])
                    late_out(i, j, spread_block(i, j), start)
                    return carry

                lax.fori_loop(1, M, late_step, 0)

        if i < S - 1:
            @pl.when(s == S - 1)
            def _():
                home(i, start)

    first_act(sent)
    for i in range(S):
        mix_act(i, sent)

        @pl.when(s > 0)
        def _():
            for c in range(len(plans[i][0])):
                hop_act(i, c, m, sent)

        @pl.when(s < S - 1)
        def _():
            hop_out(i, sent)
            if plans[i][1][1]:
                late_out(i, m, own_late(i), sent)

        if i < S - 1:
            @pl.when(s == S - 1)
            def _():
                home(i, sent)

    def drain_step(p, carry):
        j = nth(p)
        pre_act(j, sent)
        for i in range(S):
            @pl.when(s > 0)
            def _():
                for c in range(len(plans[i][0])):
                    hop_act(i, c, j, sent)

            if plans[i][1][1]:
                @pl.when(s < S - 1)
                def _():
                    late_out(i, j, spread_block(i, j), sent)

        return carry

    lax.fori_loop(1, M, drain_step, 0)

    @pl.when(s == S - 1)
    def _():
        o_ref[...] = ho[(S - 1) * L :, :]

    @pl.when(s < S - 1)
    def _():
        got(fin, fin_recv)
        o_ref[...] = fin[...]


def solution(mesh):
    S, M = mesh.shape["section"], mesh.shape["mp"]

    def shards(micro_inputs, qkv_weight, out_weight, norm_gain, position_bias):
        L, Dl = micro_inputs.shape[1:]
        D = qkv_weight.shape[1]
        Wl = qkv_weight.shape[3]
        H = position_bias.shape[0]
        R = S * L
        G = head_group(H, Wl // H)
        plans = [relay_chunks(i, S, L) for i in range(S)]
        parts = max(len(hops) for hops, _ in plans)
        late_rows = max(rows for _, (_, rows) in plans)
        buckets = jnp.asarray(bucket_table(L, position_bias.shape[1], REACH).T)
        wq = jnp.transpose(qkv_weight[0], (1, 0, 2))
        bf16, f32 = jnp.bfloat16, jnp.float32
        dma = pltpu.SemaphoreType.DMA
        vmem = pl.BlockSpec(memory_space=pltpu.VMEM)
        out = pl.pallas_call(
            functools.partial(kernel, (S, M, L, H, Wl // H)),
            out_shape=jax.ShapeDtypeStruct((L, Dl), bf16),
            in_specs=[
                vmem, vmem, vmem, pl.BlockSpec(memory_space=pltpu.SMEM),
                pl.BlockSpec(memory_space=pl.ANY), pl.BlockSpec(memory_space=pl.ANY),
            ],
            out_specs=vmem,
            scratch_shapes=[
                pltpu.VMEM((M, L, Dl), bf16),
                pltpu.VMEM((M, R, Dl), bf16),
                pltpu.VMEM((R, M * Wl), bf16),
                pltpu.VMEM((S, M, late_rows, Dl), bf16),
                pltpu.VMEM((R, Dl), bf16),
                pltpu.VMEM((L, Dl), bf16),
                pltpu.VMEM((3, D, Wl), bf16),
                pltpu.VMEM((M * Wl, Dl), bf16),
                pltpu.VMEM((L, 3 * Wl), f32),
                pltpu.VMEM((L, 128), f32),
                pltpu.VMEM((L, 3 * Wl), bf16),
                pltpu.VMEM((H // G, L, G * L), f32),
                pltpu.VMEM((G * L, Wl // H * G), bf16),
                dma((M,)), dma,
                dma((M,)), dma((2, M)), dma((M,)), dma((S, M)),
                dma((S, parts)), dma((S, parts, M)), dma((S, parts, 2, M)),
                dma((S, M)), dma((S, 2, M)), dma((S, M)), dma((S, M)),
                dma((S, M)), dma((S, M)),
                dma((S,)), dma,
            ],
            compiler_params=pltpu.CompilerParams(
                collective_id=0, has_side_effects=True, vmem_limit_bytes=60 * 1024 * 1024
            ),
        )(micro_inputs[0], norm_gain, buckets, position_bias, wq, out_weight[0])
        return out[None]

    in_specs = (
        P(("dp", "section"), None, "mp"),
        P("section", None, None, "mp"),
        P("section", None, "mp"),
        P("section", None),
        P("mp", None),
    )
    out_specs = P(("dp", "section"), None, "mp")
    return jax.shard_map(shards, mesh=mesh, in_specs=in_specs, out_specs=out_specs, check_vma=False)
```

time: 80.1 us -> 70.1 us (0.88)
  Pallas kernels: 77 us -> 68.4 us
  other arithmetic: 1.34 us -> 0 us
    pallas_call x1, Pallas kernels: 77 us -> 68.4 us  [shards(): pl.pallas_call(functools.partial(kernel, (S, M, L, H, Wl // H)), out_shap...]
    convert_element_type x1 -> x0, other arithmetic: 1.34 us -> none  [shards(): gain = norm_gain.reshape(M, 1, Dl).astype(jnp.float32)]
where the time goes in v2:
time: 70.1 us; the launch traced here: 70 us
  Pallas kernels  68.4 us (98%)
  local copies, waits for them, and re-layouts  1.57 us (2%)
    pallas_call x1, Pallas kernels, shards(): pl.pallas_call(functools.partial(kernel, (S, M, L, H, Wl // H)), out_shap...  68.4 us
    unnamed x1, local copies, waits for them, and re-layouts  1.57 us

profile of v2, /device:TPU:0, one launch (start us, length us, event | category | flops | bytes accessed | tf_op | source)
XLA Modules:
  0.0 70.0 jit_solution(3172765288924002594)
XLA Ops:
  0.0 68.4 %shard_map.64 = bf16[64,1024]{1,0:T(8,128)(2,1)} custom-call(bf16[64,1024]{1,0:T(8,128)(2,1)} %bitcast.9, bf16[1,4096]{1,0:T(2,128)(2,1)} %gain_ref.1, s32[64,64]{1,0:T(8,128)} %constant.2.clone.bucket_ref, f32[8,32]{1,0:T(8,128)} %pbias_ref.1, bf16[3,4096,512]{2,1,0:T(8,128)(2,1)} %bitcast.6, bf16[2048,1024]{1,0:T(8,128)(2,1)} %bitcast.7), custom_call_target="tpu_custom_call" | custom-call | tf_op jit(solution)/shard_map/pallas_call | solution.py:370
  68.4 1.6 %copy.8 = bf16[1,64,1024]{2,1,0:T(8,128)(2,1)} copy(bf16[1,64,1024]{2,1,0:T(8,128)(2,1)} %bitcast.8) | data formatting | bytes 262144

commit v3 on v2

--- a/solution.py
+++ b/solution.py
@@ -30,10 +30,10 @@
 
 
 def relay_chunks(micro, micros, length):
-    here = length // 2 // 16 * 16 if micro == micros - 1 else 0
-    there = length - here
-    half = max(16, there // 2 // 16 * 16)
-    return [(at, min(half, there - at)) for at in range(0, there, half)], (there, here)
+    half = length // 2
+    if micro == micros - 1:
+        return [], (0, half), (half, length - half)
+    return [(0, half), (half, length - half)], (0, 0), (0, 0)
 
 
 def head_group(heads, head_size):
@@ -48,7 +48,7 @@
     wq_sem, wo_sem,
     pre_recv, pre_send, pre_up, in_recv,
     hop_send, hop_recv, hop_line,
-    spread_recv, spread_send, spread_up, late_recv,
+    spread_recv, spread_send, spread_up, late_recv, straight_send, straight_recv,
     mix_recv, mix_send,
     fin_send, fin_recv,
 ):
@@ -69,13 +69,15 @@
         )
 
     def along(j, src, dst, send, recv, act):
-        @pl.when((j <= m) & (m < M - 1))
-        def _():
-            act(to(src, dst, send.at[0, j], recv, s, m + 1))
-
-        @pl.when((j >= m) & (m > 0))
-        def _():
-            act(to(src, dst, send.at[1, j], recv, s, m - 1))
+        even = lax.rem(m - j + 2 * M, 2) == 0
+        for reach in (2, 1):
+            @pl.when((j <= m) & even & (m < M - reach))
+            def _():
+                act(to(src, dst, send.at[reach - 1, j], recv, s, m + reach))
+
+            @pl.when((j >= m) & even & (m >= reach))
+            def _():
+                act(to(src, dst, send.at[reach + 1, j], recv, s, m - reach))
 
     def start(c):
         c.start()
@@ -102,36 +104,45 @@
         return pltpu.make_async_copy(wo_hbm, wo, wo_sem)
 
     barrier = pltpu.get_barrier_semaphore()
-    for k in range(1, M):
-        pl.semaphore_signal(
-            barrier, inc=1, device_id={"section": s, "mp": lax.rem(m + k, M)}, device_id_type=MESH
-        )
-    for k in range(1, S):
-        pl.semaphore_signal(
-            barrier, inc=1, device_id={"section": lax.rem(s + k, S), "mp": m}, device_id_type=MESH
-        )
+    for o in range(S):
+        for k in range(M):
+            if o or k:
+                pl.semaphore_signal(
+                    barrier, inc=1,
+                    device_id={"section": lax.rem(s + o, S), "mp": lax.rem(m + k, M)},
+                    device_id_type=MESH,
+                )
 
     for p in range(M):
         wq_copy(nth(p)).start()
     wo_copy().start()
-    pl.semaphore_wait(barrier, S + M - 2)
-
-    def up_rows(j):
-        return xg.at[j, pl.ds(pl.multiple_of(s * L, L), L), :]
+    pl.semaphore_wait(barrier, S * M - 1)
+
+    half = L // 2
+    halves = [pl.ds(0, half), pl.ds(half, L - half)]
+
+    def up_rows(j, c):
+        return xg.at[j, pl.ds(pl.multiple_of(s * L + c * half, half), halves[c].size), :]
+
+    def pre_part(j, c, src, act):
+        along(j, src, pre.at[j, halves[c], :], pre_send.at[c], pre_recv.at[c, j], act)
+
+        @pl.when(s > 0)
+        def _():
+            act(to(src, up_rows(j, c), pre_up.at[c, j], in_recv.at[s, c, j], 0, m))
 
     def first_act(act):
-        along(m, x_ref, pre.at[m], pre_send, pre_recv.at[m], act)
-
-        @pl.when(s > 0)
-        def _():
-            act(to(x_ref, up_rows(m), pre_up.at[m], in_recv.at[s, m], 0, m))
+        for c in range(2):
+            pre_part(m, c, x_ref.at[halves[c], :], act)
 
     def pre_act(j, act):
-        along(j, pre.at[j], pre.at[j], pre_send, pre_recv.at[j], act)
-
-        @pl.when(s > 0)
-        def _():
-            act(to(pre.at[j], up_rows(j), pre_up.at[j], in_recv.at[s, j], 0, m))
+        for c in range(2):
+            pre_part(j, c, pre.at[j, halves[c], :], act)
+
+    def pre_step_on(j):
+        for c in range(2):
+            got(pre.at[j, halves[c], :], pre_recv.at[c, j])
+            pre_part(j, c, pre.at[j, halves[c], :], start)
 
     first_act(start)
 
@@ -154,8 +165,7 @@
     def _():
         def pre_step(p, carry):
             j = nth(p)
-            got(pre.at[j], pre_recv.at[j])
-            pre_act(j, start)
+            pre_step_on(j)
             return carry
 
         lax.fori_loop(1, M, pre_step, 0)
@@ -172,6 +182,10 @@
         at, rows = plans[i][1]
         return xg.at[j, pl.ds(i * L + at, rows), :]
 
+    def straight_block(i, j):
+        at, rows = plans[i][2]
+        return xg.at[j, pl.ds(i * L + at, rows), :]
+
     def spread_block(i, j):
         return spread.at[i, j, pl.ds(0, plans[i][1][1]), :]
 
@@ -179,7 +193,8 @@
         @pl.when(s == 0)
         def _():
             if i:
-                got(xg.at[j, pl.ds(i * L, L), :], in_recv.at[i, j])
+                for c in range(2):
+                    got(xg.at[j, pl.ds(i * L + c * half, halves[c].size), :], in_recv.at[i, c, j])
             else:
                 @pl.when(j == m)
                 def _():
@@ -187,8 +202,7 @@
 
                 @pl.when(j != m)
                 def _():
-                    got(pre.at[j], pre_recv.at[j])
-                    pre_act(j, start)
+                    pre_step_on(j)
                     xg[j, 0:L, :] = pre[j]
 
         @pl.when(s > 0)
@@ -198,6 +212,8 @@
                 hop_act(i, c, j, start)
             if plans[i][1][1]:
                 got(late_block(i, j), late_recv.at[i, j])
+            if plans[i][2][1]:
+                got(straight_block(i, j), straight_recv.at[i, j])
 
     def mix_act(i, act):
         block = hg.at[pl.ds(i * L, L), pl.ds(pl.multiple_of(m * Wl, Wl), Wl)]
@@ -267,6 +283,12 @@
         along(j, src, spread_block(i, j), spread_send.at[i], spread_recv.at[i, j], act)
         act(to(src, late_block(i, j), spread_up.at[i, j], late_recv.at[i, j], s + 1, m))
 
+    def straight_out(i, act):
+        at, rows = plans[i][2]
+        for k in range(M):
+            act(to(ho.at[pl.ds(i * L + at, rows), :], straight_block(i, m),
+                   straight_send.at[i, k], straight_recv.at[i, m], s + 1, lax.rem(m + k, M)))
+
     def own_late(i):
         at, rows = plans[i][1]
         return ho.at[pl.ds(i * L + at, rows), :]
@@ -287,6 +309,9 @@
             hop_out(i, start)
             if plans[i][1][1]:
                 late_out(i, m, own_late(i), start)
+            if plans[i][2][1]:
+                straight_out(i, start)
+            if plans[i][1][1]:
 
                 def late_step(p, carry):
                     j = nth(p)
@@ -315,6 +340,8 @@
             hop_out(i, sent)
             if plans[i][1][1]:
                 late_out(i, m, own_late(i), sent)
+            if plans[i][2][1]:
+                straight_out(i, sent)
 
         if i < S - 1:
             @pl.when(s == S - 1)
@@ -360,8 +387,8 @@
         R = S * L
         G = head_group(H, Wl // H)
         plans = [relay_chunks(i, S, L) for i in range(S)]
-        parts = max(len(hops) for hops, _ in plans)
-        late_rows = max(rows for _, (_, rows) in plans)
+        parts = max(1, *(len(hops) for hops, _, _ in plans))
+        late_rows = max(rows for _, (_, rows), _ in plans)
         buckets = jnp.asarray(bucket_table(L, position_bias.shape[1], REACH).T)
         wq = jnp.transpose(qkv_weight[0], (1, 0, 2))
         bf16, f32 = jnp.bfloat16, jnp.float32
@@ -372,7 +399,7 @@
             out_shape=jax.ShapeDtypeStruct((L, Dl), bf16),
             in_specs=[
                 vmem, vmem, vmem, pl.BlockSpec(memory_space=pltpu.SMEM),
-                pl.BlockSpec(memory_space=pl.ANY), pl.BlockSpec(memory_space=pl.ANY),
+                pl.BlockSpec(memory_space=pltpu.HBM), pl.BlockSpec(memory_space=pltpu.HBM),
             ],
             out_specs=vmem,
             scratch_shapes=[
@@ -390,9 +417,9 @@
                 pltpu.VMEM((H // G, L, G * L), f32),
                 pltpu.VMEM((G * L, Wl // H * G), bf16),
                 dma((M,)), dma,
-                dma((M,)), dma((2, M)), dma((M,)), dma((S, M)),
-                dma((S, parts)), dma((S, parts, M)), dma((S, parts, 2, M)),
-                dma((S, M)), dma((S, 2, M)), dma((S, M)), dma((S, M)),
+                dma((2, M)), dma((2, 4, M)), dma((2, M)), dma((S, 2, M)),
+                dma((S, parts)), dma((S, parts, M)), dma((S, parts, 4, M)),
+                dma((S, M)), dma((S, 4, M)), dma((S, M)), dma((S, M)), dma((S, M)), dma((S, M)),
                 dma((S, M)), dma((S, M)),
                 dma((S,)), dma,
             ],

time: 70.1 us -> 64.9 us (0.926)
  Pallas kernels: 68.4 us -> 63.2 us
    pallas_call x1, Pallas kernels: 68.4 us -> 63.2 us  [shards(): pl.pallas_call(functools.partial(kernel, (S, M, L, H, Wl // H)), out_shap...]
where the time goes in v3:
time: 64.9 us; the launch traced here: 64.8 us
  Pallas kernels  63.2 us (97%)
  local copies, waits for them, and re-layouts  1.57 us (2%)
    pallas_call x1, Pallas kernels, shards(): pl.pallas_call(functools.partial(kernel, (S, M, L, H, Wl // H)), out_shap...  63.2 us
    unnamed x1, local copies, waits for them, and re-layouts  1.57 us

profile of v3, /device:TPU:0, one launch (start us, length us, event | category | flops | bytes accessed | tf_op | source)
XLA Modules:
  0.0 64.8 jit_solution(17519106335434247233)
XLA Ops:
  0.0 63.2 %shard_map.64 = bf16[64,1024]{1,0:T(8,128)(2,1)} custom-call(bf16[64,1024]{1,0:T(8,128)(2,1)} %bitcast.9, bf16[1,4096]{1,0:T(2,128)(2,1)} %gain_ref.1, s32[64,64]{1,0:T(8,128)} %constant.2.clone.bucket_ref, f32[8,32]{1,0:T(8,128)} %pbias_ref.1, bf16[3,4096,512]{2,1,0:T(8,128)(2,1)} %bitcast.6, bf16[2048,1024]{1,0:T(8,128)(2,1)} %bitcast.7), custom_call_target="tpu_custom_call" | custom-call | tf_op jit(solution)/shard_map/pallas_call | solution.py:397
  63.2 1.6 %copy.8 = bf16[1,64,1024]{2,1,0:T(8,128)(2,1)} copy(bf16[1,64,1024]{2,1,0:T(8,128)(2,1)} %bitcast.8) | data formatting | bytes 262144

commit v4 on v3

--- a/solution.py
+++ b/solution.py
@@ -217,9 +217,8 @@
 
     def mix_act(i, act):
         block = hg.at[pl.ds(i * L, L), pl.ds(pl.multiple_of(m * Wl, Wl), Wl)]
-        for k in range(1, M):
-            col = lax.rem(m + k, M)
-            act(to(block, block, mix_send.at[i, k], mix_recv.at[i, m], s, col))
+        for p in reversed(range(1, M)):
+            act(to(block, block, mix_send.at[i, p], mix_recv.at[i, m], s, nth(p)))
 
     scale = 1.0 / math.sqrt(hs)
     lane_head = lax.broadcasted_iota(jnp.int32, (L, Wg), 1) // hs
@@ -285,9 +284,9 @@
 
     def straight_out(i, act):
         at, rows = plans[i][2]
-        for k in range(M):
+        for p in reversed(range(M)):
             act(to(ho.at[pl.ds(i * L + at, rows), :], straight_block(i, m),
-                   straight_send.at[i, k], straight_recv.at[i, m], s + 1, lax.rem(m + k, M)))
+                   straight_send.at[i, p], straight_recv.at[i, m], s + 1, nth(p)))
 
     def own_late(i):
         at, rows = plans[i][1]

time: 64.9 us -> 66.9 us (1.031)
  Pallas kernels: 63.2 us -> 65.1 us
    pallas_call x1, Pallas kernels: 63.2 us -> 65.1 us  [shards(): pl.pallas_call(functools.partial(kernel, (S, M, L, H, Wl // H)), out_shap...]
where the time goes in v4:
time: 66.9 us; the launch traced here: 66.7 us
  Pallas kernels  65.1 us (97%)
  local copies, waits for them, and re-layouts  1.57 us (2%)
    pallas_call x1, Pallas kernels, shards(): pl.pallas_call(functools.partial(kernel, (S, M, L, H, Wl // H)), out_shap...  65.1 us
    unnamed x1, local copies, waits for them, and re-layouts  1.57 us

profile of v4, /device:TPU:0, one launch (start us, length us, event | category | flops | bytes accessed | tf_op | source)
XLA Modules:
  0.0 66.7 jit_solution(10397393641407886736)
XLA Ops:
  0.0 65.1 %shard_map.64 = bf16[64,1024]{1,0:T(8,128)(2,1)} custom-call(bf16[64,1024]{1,0:T(8,128)(2,1)} %bitcast.9, bf16[1,4096]{1,0:T(2,128)(2,1)} %gain_ref.1, s32[64,64]{1,0:T(8,128)} %constant.2.clone.bucket_ref, f32[8,32]{1,0:T(8,128)} %pbias_ref.1, bf16[3,4096,512]{2,1,0:T(8,128)(2,1)} %bitcast.6, bf16[2048,1024]{1,0:T(8,128)(2,1)} %bitcast.7), custom_call_target="tpu_custom_call" | custom-call | tf_op jit(solution)/shard_map/pallas_call | solution.py:396
  65.1 1.6 %copy.8 = bf16[1,64,1024]{2,1,0:T(8,128)(2,1)} copy(bf16[1,64,1024]{2,1,0:T(8,128)(2,1)} %bitcast.8) | data formatting | bytes 262144
